TPU v7x, 32 devices: a whole 2x2x4 slice. The times are simulated.
32 devices in a mesh: groups: 2 (over y), gx: 4 (over z), gy: 4 (over x, core).
Axes of the slice: x: 2, y: 2, z: 4, core: 2. Of those that a mesh axis runs over, the one named last changes fastest.
Arguments:
- tokens: bfloat16 [2, 16, 16384], P(None, 'groups', 'gx'), parts along dimension 1, may hold values from -20 to 20, as said below
- lengths: int32 [2, 16], P(None, ('groups', 'gx')), parts along dimension 1, may hold values from 1 to 1024, as said below
- norm_gain: bfloat16 [16384], P('gx'), may hold values from 0.5 to 2
- w_query: bfloat16 [16384, 8192], P('gx', 'gy'), may hold values from -1.171875 to 1.171875
- key_value_weight: bfloat16 [16384, 4, 256], P('gx', 'gy'), may hold values from -0.046875 to 0.046875
- w_out: bfloat16 [8192, 16384], P('gy', 'gx'), may hold values from -0.0625 to 0.0625
- cache: bfloat16 [2, 16, 1024, 4, 2, 128], P(None, ('groups', 'gx'), None, 'gy'), parts along dimension 1, may hold values from -16 to 16
Outputs:
- layer_out: bfloat16 [2, 16, 16384], P(None, 'groups', 'gx'), parts along dimension 1
There are 2 independent parts, one for each index of `groups`. A program takes and returns all parts, laid end to end along the dimension named above; an argument that names none is the same for every part. Nothing has to cross between parts.
Inputs may be any that keep to these rules, and one draw needn't show every extreme that they name: `tokens`: entries vary with the feature and the row. `lengths`: some rollout has exactly 1024 cached positions in every draw.
All inputs are finite; a program needn't handle non-finite values.
Results may differ from a plain program's by a relative error of at most 0.012.
The roundings to bfloat16 on the way count: a program that leaves them out, or rounds other values in their place, can miss the bound.
Values may be sent and summed in bfloat16 or wider, within the bound.
No kernel may reach another device: no remote copies, remote signals or barrier semaphores. Data moves between devices by JAX's collectives and lax.ppermute only.
A program may use at most 128 MiB of HBM per device.

v0:
```python
import jax
import jax.numpy as jnp
from jax import lax
from jax.sharding import PartitionSpec as P

MODEL_WIDTH = 16384
HEAD_SIZE = 128


def rotate(vectors, positions):
    half = vectors.shape[-1] // 2
    freq = 500000.0 ** (-2.0 * jnp.arange(half, dtype=jnp.float32) / vectors.shape[-1])
    angle = positions[..., None] * freq
    cosine = jnp.cos(angle)
    sine = jnp.sin(angle)
    first = vectors[..., :half]
    second = vectors[..., half:]
    return jnp.concatenate(
        [first * cosine - second * sine, second * cosine + first * sine], axis=-1
    )


def attend(query_sum, keyval_sum, local_squares, lengths, cache):
    batches, rows_here = lengths.shape
    score_scale = lax.rsqrt(local_squares / MODEL_WIDTH + 1e-05)
    heads_kv = keyval_sum.shape[2]
    query_group = query_sum.shape[2] // (heads_kv * HEAD_SIZE)
    query = (
        query_sum.reshape(batches, rows_here, heads_kv, query_group, HEAD_SIZE)
        * score_scale[:, :, None, None, None]
    )
    key_value = keyval_sum * score_scale[:, :, None, None]
    positions = lengths.astype(jnp.float32)
    rotated_query = rotate(query, positions[:, :, None, None]).astype(jnp.bfloat16)
    rkey = rotate(key_value[..., :HEAD_SIZE], positions[:, :, None])
    value_new = key_value[..., HEAD_SIZE:]
    inv_root = 1.0 / jnp.sqrt(jnp.float32(HEAD_SIZE))
    keys = cache[:, :, :, :, 0, :]
    values = cache[:, :, :, :, 1, :]
    scores = (
        jnp.einsum("mrkgd,mrskd->mrkgs", rotated_query, keys, preferred_element_type=jnp.float32)
        * inv_root
    )
    valid = jnp.arange(cache.shape[2], dtype=jnp.int32)[None, None, :] < lengths[:, :, None]
    scores = jnp.where(valid[:, :, None, None, :], scores, -1e30)
    new_score = (
        jnp.sum(rotated_query.astype(jnp.float32) * rkey[:, :, :, None, :], axis=-1) * inv_root
    )
    top = jnp.maximum(jnp.max(scores, axis=-1), new_score)
    weights = jnp.exp(scores - top[..., None])
    new_weight = jnp.exp(new_score - top)
    total = jnp.sum(weights, axis=-1) + new_weight
    summed = jnp.einsum(
        "mrkgs,mrskd->mrkgd",
        weights.astype(jnp.bfloat16),
        values,
        preferred_element_type=jnp.float32,
    )
    summed = summed + new_weight[..., None] * value_new[:, :, :, None, :]
    return (
        (summed / total[..., None])
        .astype(jnp.bfloat16)
        .reshape(batches, rows_here, heads_kv * query_group * HEAD_SIZE)
    )


def local(tokens, lengths, norm_gain, w_query, key_value_weight, w_out, cache):
    x_full = tokens.astype(jnp.float32)
    squares = jnp.sum(x_full * x_full, axis=-1)
    normed = (x_full * norm_gain.astype(jnp.float32)).astype(jnp.bfloat16)
    query_part = jnp.einsum("mrd,dc->mrc", normed, w_query, preferred_element_type=jnp.float32)
    keyval_part = jnp.einsum(
        "mrd,dkc->mrkc", normed, key_value_weight, preferred_element_type=jnp.float32
    )
    query_sum, keyval_sum, local_squares = (
        lax.psum_scatter(query_part, "gx", scatter_dimension=1, tiled=True),
        lax.psum_scatter(keyval_part, "gx", scatter_dimension=1, tiled=True),
        lax.psum_scatter(squares, "gx", scatter_dimension=1, tiled=True),
    )
    attended = attend(query_sum, keyval_sum, local_squares, lengths, cache)
    projected = jnp.einsum(
        "mrc,cd->mrd",
        lax.all_gather(attended, "gx", axis=1, tiled=True),
        w_out,
        preferred_element_type=jnp.float32,
    )
    summed_heads = lax.psum(projected, "gy")
    return (x_full + summed_heads).astype(jnp.bfloat16)


def solution(mesh):
    placed = (
        P(None, "groups", "gx"),
        P(None, ("groups", "gx")),
        P("gx"),
        P("gx", "gy"),
        P("gx", "gy", None),
        P("gy", "gx"),
        P(None, ("groups", "gx"), None, "gy", None, None),
    )
    return jax.shard_map(
        local, mesh=mesh, in_specs=placed, out_specs=P(None, "groups", "gx"), check_vma=False
    )
```

profile of v0, /device:TPU:0, one launch (start us, length us, event | category | flops | bytes accessed | tf_op | source)
XLA Modules:
  0.0 122.0 jit_solution(11372717634072038642)
XLA Ops:
  6.5 0.0 copy-start
  6.5 0.0 all-reduce.9.cloned.1.call-start
  6.5 0.8 convert_element_type.46
  7.4 8.8 %fusion.2 = f32[2,8,2048]{2,1,0:T(8,128)} fusion(bf16[4096,2048]{1,0:T(8,128)(2,1)} %param.10, bf16[2,8,4096]{2,1,0:T(8,128)(2,1)} %param.7, f32[4096]{0:T(1024)S(1)} %convert_element_type.46), kind=kOutput, calls=%fused_computation.2 | convolution fusion | flops 268632064 | bytes 17055744 | tf_op jit(solution)/shard_map/mrd,dc->mrc/dot_general | solution.py:71
  16.2 0.0 all-reduce.9.cloned.1.call-update
  16.2 0.0 all-reduce.7.cloned.1.call-start
  16.3 0.1 fusion.13
  16.4 0.0 copy-done.2
  16.4 0.1 iota_compare_fusion
  16.5 0.0 copy-done
  16.5 0.4 fusion.9
  16.9 0.7 dynamic-slice
  18.3 0.1 multiply_cosine_fusion.1
  18.4 20.8 %all-reduce.3 = (f32[2,8]{1,0:T(2,128)S(1)}, f32[2,8,1,256]{3,1,0,2:T(8,128)S(1)}) all-reduce(f32[2,8]{1,0:T(2,128)S(1)} %fusion.13, f32[2,8,1,256]{3,1,0,2:T(8,128)S(1)} %fusion.9), channel_id=3, replica_groups=mesh['groups'=2,'gx'=4,'gy'=4] {'gx'}, use_global_device_ids=true, to_apply=%region_2.0.clone | all-reduce | flops 4112 | bytes 32896
  39.2 0.1 fusion.32
  39.3 0.1 dynamic-slice_multiply_fusion
  39.4 0.1 fusion.29
  39.5 6.9 %fusion.35 = (bf16[2,2,1024,1,1,128]{5,4,3,2,1,0:T(2,128)(2,1)}, bf16[2,2,1024,1,1,128]{5,4,3,2,1,0:T(2,128)(2,1)}) fusion(bf16[2,2,1024,1,2,128]{5,4,3,2,1,0:T(2,128)(2,1)} %param.13), kind=kLoop, calls=%fused_computation.55 | loop fusion | bytes 4194304 | tf_op jit(solution)/shard_map/slice | solution.py:38
  46.4 0.1 maximum_bitcast_fusion
  46.5 7.3 %all-reduce.9.cloned.1.call-done = f32[2,8,2048]{2,1,0:T(8,128)} async-done(((f32[2,8,2048]{2,1,0:T(8,128)}), f32[2,8,2048]{2,1,0:T(8,128)}) %all-reduce.9.cloned.1.call-update) | async-done | bytes 131088
  53.9 0.9 constant_dynamic-slice_fusion
  54.8 0.1 broadcast_multiply_fusion
  54.9 0.1 subtract_convert_fusion
  55.0 0.2 multiply_reduce_fusion
  55.1 2.1 %fusion.36 = (f32[2,2,16]{2,1,0:T(2,128)S(1)}, f32[2,2,16,1024]{3,2,1,0:T(8,128)S(1)}) fusion(bf16[2,2,1024,1,1,128]{5,4,3,2,1,0:T(2,128)(2,1)} %get-tuple-element.9, bf16[2,2,16,64]{3,2,1,0:T(8,128)(2,1)S(1)} %bitcast.38, bf16[2,2,16,64]{3,2,1,0:T(8,128)(2,1)S(1)} %bitcast.37, pred[2,2,1024]{2,1,0:T(4,128)(4,1)S(1)} %iota_compare_fusion), kind=kOutput, calls=%fused_computation.56 | convolution fusion | flops 17006528 | bytes 1331456 | tf_op jit(solution)/shard_map/mrkgd,mrskd->mrkgs/dot_general | solution.py:41
  57.3 0.2 fusion.15
  57.5 1.9 %fusion.8 = bf16[2,2,16,128]{3,2,1,0:T(8,128)(2,1)S(1)} fusion(bf16[2,2,1024,1,1,128]{5,4,3,2,1,0:T(2,128)(2,1)} %get-tuple-element.10, f32[2,2,16,1024]{3,2,1,0:T(8,128)S(1)} %get-tuple-element.18, f32[2,2,16]{2,1,0:T(2,128)S(1)} %multiply_maximum_fusion, f32[2,2,16]{2,1,0:T(2,128)S(1)} %get-tuple-element.7, f32[2,2,128]{2,1,0:T(2,128)S(1)} %slice_bitcast_fusion, ...), kind=kOutput, calls=%fused_computation.10 | convolution fusion | flops 16941056 | bytes 1329920 | tf_op jit(solution)/shard_map/mrkgs,mrskd->mrkgd/dot_general | solution.py:53
  59.4 13.1 %all_gather.3 = bf16[2,8,2048]{2,0,1:T(2,128)(2,1)S(1)} all-gather(bf16[2,2,2048]{2,0,1:T(2,128)(2,1)S(1)} %copy.12), channel_id=1, replica_groups=mesh['groups'=2,'gx'=4,'gy'=4] {'gx'}, dimensions={1}, use_global_device_ids=true | all-gather | bytes 81920 | tf_op jit(solution)/shard_map/all_gather | solution.py:83
  72.6 8.8 %fusion = f32[2,8,4096]{2,1,0:T(8,128)} fusion(bf16[2048,4096]{1,0:T(8,128)(2,1)} %param.12, bf16[2,8,2048]{2,0,1:T(2,128)(2,1)S(1)} %all_gather.3), kind=kOutput, calls=%fused_computation | convolution fusion | flops 268435456 | bytes 17104896 | tf_op jit(solution)/shard_map/mrc,cd->mrd/dot_general | solution.py:81
  81.3 0.0 all-reduce.7.cloned.1.call-update
  81.3 32.2 %all-reduce.7.cloned.1.call-done = f32[2,8,4096]{2,1,0:T(8,128)} async-done(((f32[2,8,4096]{2,1,0:T(8,128)}), f32[2,8,4096]{2,1,0:T(8,128)}) %all-reduce.7.cloned.1.call-update) | async-done | bytes 262160 | tf_op jit(solution)/shard_map/psum | solution.py:87
  113.5 1.6 %fusion.14 = bf16[2,8,4096]{2,1,0:T(8,128)(2,1)} fusion(f32[2,8,4096]{2,1,0:T(8,128)} %all-reduce.7.cloned.1.call-done, bf16[2,8,4096]{2,1,0:T(8,128)(2,1)S(1)} %copy-done.1), kind=kLoop, calls=%fused_computation.19 | loop fusion | flops 196608 | bytes 524288 | tf_op jit(solution)/shard_map/convert_element_type | solution.py:88
  (13 shorter events, 0.1 us)
Async XLA Ops:
  6.5 10.0 %copy-start = (bf16[4096,1,256]{2,0,1:T(8,128)(2,1)S(1)}, bf16[4096,1,256]{2,0,1:T(8,128)(2,1)}, u32[]{:S(2)}) copy-start(bf16[4096,1,256]{2,0,1:T(8,128)(2,1)} %param.11) | copy-start | bytes 6291460
  6.5 47.3 %all-reduce.9.cloned.1.call-start = ((), (), s32[]{:S(2)}) async-start(), calls=%async_computation.1 | async-start | bytes 262144
  7.4 8.9 %copy-start.1 = (bf16[2,8,4096]{2,1,0:T(8,128)(2,1)S(1)}, bf16[2,8,4096]{2,1,0:T(8,128)(2,1)}, u32[]{:S(2)}) copy-start(bf16[2,8,4096]{2,1,0:T(8,128)(2,1)} %param.7) | copy-start | bytes 393220
  7.4 9.0 %copy-start.2 = (s32[2,2]{1,0:T(2,128)S(1)}, s32[2,2]{1,0:T(2,128)}, u32[]{:S(2)}) copy-start(s32[2,2]{1,0:T(2,128)} %param.8) | copy-start | bytes 52
  16.2 0.7 copy-start.3
  16.2 97.3 %all-reduce.7.cloned.1.call-start = ((), (), s32[]{:S(2)}) async-start(), calls=%async_computation | async-start | bytes 524288 | tf_op jit(solution)/shard_map/psum | solution.py:87
Sparse Core Ops, SparseCore 0:
  16.4 37.4 all-reduce.8
  81.5 31.9 all-reduce.6
where the time goes:
time: 122 us
  waiting for transfers between devices  39.5 us (32%)
  blocking collectives  33.9 us (28%)
  matrix products  22 us (18%)
  between operations  14.2 us (12%)
  local copies, waits for them, and re-layouts  8.61 us (7%)
  other arithmetic  3.71 us (3%)
    psum x1, waiting for transfers between devices, local(): summed_heads = lax.psum(projected, 'gy')  32.2 us
    unnamed x1, blocking collectives  20.8 us
    all_gather x1, blocking collectives, local(): lax.all_gather(attended, 'gx', axis=1, tiled=True)  13.1 us
    dot_general x1, matrix products, local(): jnp.einsum('mrd,dc->mrc', normed, w_query, preferred_element_type=jnp.flo...  8.81 us
    dot_general x1, matrix products, local(): jnp.einsum('mrc,cd->mrd', lax.all_gather(attended, 'gx', axis=1, tiled=Tr...  8.75 us
    unnamed x3, waiting for transfers between devices  7.38 us
    slice x1, local copies, waits for them, and re-layouts, attend(): keys = cache[:, :, :, :, 0, :]  6.95 us
  transfers between devices with their start and end apart: 2, of which 2 were waited for; matrix products, arithmetic and copies ran while one was open for 7% of the time, Pallas kernels for 0%

commit v1 on v0

--- a/solution.py
+++ b/solution.py
@@ -5,6 +5,12 @@
 
 MODEL_WIDTH = 16384
 HEAD_SIZE = 128
+
+
+def in_order(tiles, dim):
+    tiles = jnp.moveaxis(tiles, 0, dim)
+    dims = tiles.shape
+    return tiles.reshape(*dims[:dim], dims[dim] * dims[dim + 1], *dims[dim + 2 :])
 
 
 def rotate(vectors, positions):
@@ -78,12 +84,16 @@
         lax.psum_scatter(squares, "gx", scatter_dimension=1, tiled=True),
     )
     attended = attend(query_sum, keyval_sum, local_squares, lengths, cache)
-    projected = jnp.einsum(
-        "mrc,cd->mrd",
-        lax.all_gather(attended, "gx", axis=1, tiled=True),
-        w_out,
-        preferred_element_type=jnp.float32,
-    )
+    length, mine, width = (lax.axis_size("gx"), lax.axis_index("gx"), attended.shape[1])
+    ahead = [(i, (i + 1) % length) for i in range(length)]
+    pieces = []
+    carried = attended
+    for step in range(length):
+        upcoming = carried if step == length - 1 else lax.ppermute(carried, "gx", ahead)
+        pieces.append(jnp.einsum("mrc,cd->mrd", carried, w_out, preferred_element_type=jnp.float32))
+        carried = upcoming
+    pieces = jnp.stack(pieces)[(mine - jnp.arange(length)) % length]
+    projected = in_order(pieces, 1)
     summed_heads = lax.psum(projected, "gy")
     return (x_full + summed_heads).astype(jnp.bfloat16)
 

time: 122 us -> 130 us (1.066)
  matrix products: 22 us -> 35.7 us
  blocking collectives: 33.9 us -> 21.2 us
  starting transfers between devices: 0.04 us -> 3.07 us
  local copies, waits for them, and re-layouts: 8.61 us -> 10.4 us
  waiting for transfers between devices: 39.5 us -> 41.1 us
    dot_general x1 -> x4, matrix products: 8.75 us -> 22.5 us  [local(): jnp.einsum('mrc,cd->mrd', carried, w_out, preferred_element_type=jnp.floa...]
    all_gather x1 -> x0, blocking collectives: 13.1 us -> none  [local(): lax.all_gather(attended, 'gx', axis=1, tiled=True)]
    ppermute x0 -> x3, waiting for transfers between devices: none -> 3.03 us  [local(): lax.ppermute(carried, 'gx', ahead)]
    ppermute x0 -> x3, starting transfers between devices: none -> 3 us  [local(): lax.ppermute(carried, 'gx', ahead)]
  transfers between devices with their start and end apart: 2 -> 5, of which waited for: 2 -> 3; matrix products, arithmetic and copies ran while one was open for 7% -> 22% of each run, Pallas kernels for 0% -> 0%
where the time goes in v1:
time: 130 us; the launch traced here: 129 us
  waiting for transfers between devices  41.1 us (32%)
  matrix products  35.7 us (27%)
  blocking collectives  21.2 us (16%)
  between operations  14.2 us (11%)
  local copies, waits for them, and re-layouts  10.4 us (8%)
  other arithmetic  3.86 us (3%)
  starting transfers between devices  3.07 us (2%)
    psum x1, waiting for transfers between devices, local(): summed_heads = lax.psum(projected, 'gy')  30.9 us
    dot_general x4, matrix products, local(): jnp.einsum('mrc,cd->mrd', carried, w_out, preferred_element_type=jnp.floa...  22.5 us
    unnamed x1, blocking collectives  21.2 us
    dot_general x1, matrix products, local(): jnp.einsum('mrd,dc->mrc', normed, w_query, preferred_element_type=jnp.flo...  8.78 us
    unnamed x3, waiting for transfers between devices  7.13 us
    slice x1, local copies, waits for them, and re-layouts, attend(): keys = cache[:, :, :, :, 0, :]  6.89 us
    ppermute x3, waiting for transfers between devices, local(): lax.ppermute(carried, 'gx', ahead)  3.03 us
    ppermute x3, starting transfers between devices, local(): lax.ppermute(carried, 'gx', ahead)  3 us
  transfers between devices with their start and end apart: 5, of which 3 were waited for; matrix products, arithmetic and copies ran while one was open for 22% of the time, Pallas kernels for 0%

profile of v1, /device:TPU:0, one launch (start us, length us, event | category | flops | bytes accessed | tf_op | source)
XLA Modules:
  0.0 129.4 jit_solution(12856610856104826365)
XLA Ops:
  6.6 0.8 convert_element_type.46
  7.4 8.8 %fusion.8 = f32[2,8,2048]{2,1,0:T(8,128)} fusion(bf16[4096,2048]{1,0:T(8,128)(2,1)} %param.10, bf16[2,8,4096]{2,1,0:T(8,128)(2,1)} %param.7, f32[4096]{0:T(1024)S(1)} %convert_element_type.46), kind=kOutput, calls=%fused_computation.9 | convolution fusion | flops 268632064 | bytes 17055744 | tf_op jit(solution)/shard_map/mrd,dc->mrc/dot_general | solution.py:77
  16.3 0.1 fusion.31
  16.4 0.1 iota_compare_fusion
  16.5 0.4 fusion.27
  16.9 21.2 %all-reduce.3 = (f32[2,8]{1,0:T(2,128)S(1)}, f32[2,8,1,256]{3,1,0,2:T(8,128)S(1)}) all-reduce(f32[2,8]{1,0:T(2,128)S(1)} %fusion.31, f32[2,8,1,256]{3,1,0,2:T(8,128)S(1)} %fusion.27), channel_id=3, replica_groups=mesh['groups'=2,'gx'=4,'gy'=4] {'gx'}, use_global_device_ids=true, to_apply=%region_2.0.clone | all-reduce | flops 4112 | bytes 32896
  38.1 0.6 dynamic-slice
  39.4 0.1 dynamic-slice_multiply_fusion
  39.4 0.1 multiply_cosine_fusion.1
  39.6 0.1 fusion.46
  39.7 6.9 %fusion.54 = (bf16[2,2,1024,1,1,128]{5,4,3,2,1,0:T(2,128)(2,1)}, bf16[2,2,1024,1,1,128]{5,4,3,2,1,0:T(2,128)(2,1)}) fusion(bf16[2,2,1024,1,2,128]{5,4,3,2,1,0:T(2,128)(2,1)} %param.13), kind=kLoop, calls=%fused_computation.73 | loop fusion | bytes 4194304 | tf_op jit(solution)/shard_map/slice | solution.py:44
  46.7 7.1 %all-reduce.9.cloned.1.call-done = f32[2,8,2048]{2,1,0:T(8,128)} async-done(((f32[2,8,2048]{2,1,0:T(8,128)}), f32[2,8,2048]{2,1,0:T(8,128)}) %all-reduce.9.cloned.1.call-update) | async-done | bytes 131088
  53.8 0.9 constant_dynamic-slice_fusion
  54.8 0.1 subtract_convert_fusion
  54.9 0.2 multiply_reduce_fusion
  55.1 2.1 %fusion.55 = (f32[2,2,16]{2,1,0:T(2,128)S(1)}, f32[2,2,16,1024]{3,2,1,0:T(8,128)S(1)}) fusion(bf16[2,2,1024,1,1,128]{5,4,3,2,1,0:T(2,128)(2,1)} %get-tuple-element.9, bf16[2,2,16,64]{3,2,1,0:T(8,128)(2,1)S(1)} %bitcast.72, bf16[2,2,16,64]{3,2,1,0:T(8,128)(2,1)S(1)} %bitcast.71, pred[2,2,1024]{2,1,0:T(4,128)(4,1)S(1)} %iota_compare_fusion), kind=kOutput, calls=%fused_computation.74 | convolution fusion | flops 17006528 | bytes 1331456 | tf_op jit(solution)/shard_map/mrkgd,mrskd->mrkgs/dot_general | solution.py:47
  57.2 0.2 fusion.33
  57.4 1.9 %fusion.26 = bf16[2,2,16,128]{3,2,1,0:T(8,128)(2,1)S(1)} fusion(bf16[2,2,1024,1,1,128]{5,4,3,2,1,0:T(2,128)(2,1)} %get-tuple-element.10, f32[2,2,16,1024]{3,2,1,0:T(8,128)S(1)} %get-tuple-element.18, f32[2,2,16]{2,1,0:T(2,128)S(1)} %multiply_maximum_fusion, f32[2,2,16]{2,1,0:T(2,128)S(1)} %get-tuple-element.7, f32[2,2,128]{2,1,0:T(2,128)S(1)} %slice_bitcast_fusion, ...), kind=kOutput, calls=%fused_computation.21 | convolution fusion | flops 16941056 | bytes 1329920 | tf_op jit(solution)/shard_map/mrkgs,mrskd->mrkgd/dot_general | solution.py:59
  59.4 1.5 %collective-permute-start = (bf16[2,2,2048]{2,1,0:T(2,128)(2,1)S(1)}, bf16[2,2,2048]{2,1,0:T(2,128)(2,1)S(1)}, u32[]{:S(2)}, u32[]{:S(2)}) collective-permute-start(bf16[2,2,2048]{2,1,0:T(2,128)(2,1)S(1)} %reshape.251), channel_id=1, source_target_pairs={{0,4},{4,8},{8,12},{12,0},{1,5},{5,9},{9,13},{13,1},{2,6},{6,10},{... | collective-permute-start | bytes 49160 | tf_op jit(solution)/shard_map/ppermute | solution.py:92
  60.8 8.8 %fusion.10 = f32[1,2,2,4096]{3,2,1,0:T(2,128)S(1)} fusion(bf16[2,2,2048]{2,1,0:T(2,128)(2,1)S(1)} %reshape.251, bf16[2048,4096]{1,0:T(8,128)(2,1)} %param.12), kind=kOutput, calls=%fused_computation.11 | convolution fusion | flops 67108864 | bytes 16859136 | tf_op jit(solution)/shard_map/mrc,cd->mrd/dot_general | solution.py:93
  69.7 1.3 collective-permute-start.1
  71.0 8.8 %fusion.13 = f32[1,2,2,4096]{3,2,1,0:T(2,128)S(1)} fusion(bf16[2,2,2048]{2,1,0:T(2,128)(2,1)S(1)} %collective-permute-done, bf16[2048,4096]{1,0:T(8,128)(2,1)} %param.12), kind=kOutput, calls=%fused_computation.12 | convolution fusion | flops 67108864 | bytes 16859136 | tf_op jit(solution)/shard_map/mrc,cd->mrd/dot_general | solution.py:93
  79.7 0.3 collective-permute-start.2
  80.0 2.5 %fusion.16 = f32[1,2,2,4096]{3,2,1,0:T(2,128)S(1)} fusion(bf16[2,2,2048]{2,1,0:T(2,128)(2,1)S(1)} %collective-permute-done.1, bf16[2048,4096]{1,0:T(8,128)(2,1)S(1)} %bitcast.68), kind=kOutput, calls=%fused_computation.13 | convolution fusion | flops 67108864 | bytes 16859136 | tf_op jit(solution)/shard_map/mrc,cd->mrd/dot_general | solution.py:93
  82.5 3.0 %collective-permute-done.2 = bf16[2,2,2048]{2,1,0:T(2,128)(2,1)S(1)} collective-permute-done((bf16[2,2,2048]{2,1,0:T(2,128)(2,1)S(1)}, bf16[2,2,2048]{2,1,0:T(2,128)(2,1)S(1)}, u32[]{:S(2)}, u32[]{:S(2)}) %collective-permute-start.2) | collective-permute-done | bytes 16416 | tf_op jit(solution)/shard_map/ppermute | solution.py:92
  85.5 2.5 %fusion.19 = f32[1,2,2,4096]{3,2,1,0:T(2,128)S(1)} fusion(bf16[2,2,2048]{2,1,0:T(2,128)(2,1)S(1)} %collective-permute-done.2, bf16[2048,4096]{1,0:T(8,128)(2,1)S(1)} %bitcast.68), kind=kOutput, calls=%fused_computation.14 | convolution fusion | flops 67108864 | bytes 16859136 | tf_op jit(solution)/shard_map/mrc,cd->mrd/dot_general | solution.py:93
  88.0 0.1 pad_maximum_fusion
  88.1 0.8 gather_fusion
  88.9 0.2 copy.29
  89.2 0.9 copy.30
  90.0 30.9 %all-reduce.7.cloned.1.call-done = f32[2,8,4096]{2,1,0:T(8,128)} async-done(((f32[2,8,4096]{2,1,0:T(8,128)}), f32[2,8,4096]{2,1,0:T(8,128)}) %all-reduce.7.cloned.1.call-update) | async-done | bytes 262160 | tf_op jit(solution)/shard_map/psum | solution.py:97
  120.9 1.6 %fusion.32 = bf16[2,8,4096]{2,1,0:T(8,128)(2,1)} fusion(f32[2,8,4096]{2,1,0:T(8,128)} %all-reduce.7.cloned.1.call-done, bf16[2,8,4096]{2,1,0:T(8,128)(2,1)S(1)} %copy-done.1), kind=kLoop, calls=%fused_computation.30 | loop fusion | flops 196608 | bytes 524288 | tf_op jit(solution)/shard_map/convert_element_type | solution.py:98
  (35 shorter events, 0.5 us)
Async XLA Ops:
  6.5 10.0 %copy-start = (bf16[4096,1,256]{2,0,1:T(8,128)(2,1)S(1)}, bf16[4096,1,256]{2,0,1:T(8,128)(2,1)}, u32[]{:S(2)}) copy-start(bf16[4096,1,256]{2,0,1:T(8,128)(2,1)} %param.11) | copy-start | bytes 6291460
  6.5 31.6 %copy-start.3 = (u32[32]{0:T(128)S(1)}, u32[32]{0:T(128)}, u32[]{:S(2)}) copy-start(u32[32]{0:T(128)} %constant.49) | copy-start | bytes 388
  6.5 9.7 %copy-start.1 = (bf16[2,8,4096]{2,1,0:T(8,128)(2,1)S(1)}, bf16[2,8,4096]{2,1,0:T(8,128)(2,1)}, u32[]{:S(2)}) copy-start(bf16[2,8,4096]{2,1,0:T(8,128)(2,1)} %param.7) | copy-start | bytes 393220
  6.5 9.9 %copy-start.2 = (s32[2,2]{1,0:T(2,128)S(1)}, s32[2,2]{1,0:T(2,128)}, u32[]{:S(2)}) copy-start(s32[2,2]{1,0:T(2,128)} %param.8) | copy-start | bytes 52
  6.5 47.2 %all-reduce.9.cloned.1.call-start = ((), (), s32[]{:S(2)}) async-start(), calls=%async_computation.1 | async-start | bytes 262144
  16.2 104.7 %all-reduce.7.cloned.1.call-start = ((), (), s32[]{:S(2)}) async-start(), calls=%async_computation | async-start | bytes 524288 | tf_op jit(solution)/shard_map/psum | solution.py:97
  59.3 20.7 %slice-start = ((s8[16777216]{0:T(1024)(128)(4,1)}), s8[4194304]{0:T(1024)(128)(4,1)S(1)}, s32[]{:S(2)}) async-start(s8[16777216]{0:T(1024)(128)(4,1)} %bitcast.67), calls=%async_computation.2 | async-start | bytes 8388608
  59.4 20.7 %slice-start.1 = ((s8[16777216]{0:T(1024)(128)(4,1)}), s8[4194304]{0:T(1024)(128)(4,1)S(1)}, s32[]{:S(2)}) async-start(s8[16777216]{0:T(1024)(128)(4,1)} %bitcast.67), calls=%async_computation.3 | async-start | bytes 8388608
  59.4 10.3 %collective-permute-start = (bf16[2,2,2048]{2,1,0:T(2,128)(2,1)S(1)}, bf16[2,2,2048]{2,1,0:T(2,128)(2,1)S(1)}, u32[]{:S(2)}, u32[]{:S(2)}) collective-permute-start(bf16[2,2,2048]{2,1,0:T(2,128)(2,1)S(1)} %reshape.251), channel_id=1, source_target_pairs={{0,4},{4,8},{8,12},{12,0},{1,5},{5,9},{9,13},{13,1},{2,6},{6,10},{... | collective-permute-start | bytes 49160 | tf_op jit(solution)/shard_map/ppermute | solution.py:92
  69.6 10.4 %slice-start.2 = ((s8[16777216]{0:T(1024)(128)(4,1)}), s8[4194304]{0:T(1024)(128)(4,1)S(1)}, s32[]{:S(2)}) async-start(s8[16777216]{0:T(1024)(128)(4,1)} %bitcast.67), calls=%async_computation.4 | async-start | bytes 8388608
  69.7 10.4 %slice-start.3 = ((s8[16777216]{0:T(1024)(128)(4,1)}), s8[4194304]{0:T(1024)(128)(4,1)S(1)}, s32[]{:S(2)}) async-start(s8[16777216]{0:T(1024)(128)(4,1)} %bitcast.67), calls=%async_computation.5 | async-start | bytes 8388608
  69.7 10.0 %collective-permute-start.1 = (bf16[2,2,2048]{2,1,0:T(2,128)(2,1)S(1)}, bf16[2,2,2048]{2,1,0:T(2,128)(2,1)S(1)}, u32[]{:S(2)}, u32[]{:S(2)}) collective-permute-start(bf16[2,2,2048]{2,1,0:T(2,128)(2,1)S(1)} %collective-permute-done), channel_id=1, source_target_pairs={{0,4},{4,8},{8,12},{12,0},{1,5},{5,9},{9,13},{13,1},{2,6},{6,10},{... | collective-permute-start | bytes 49160 | tf_op jit(solution)/shard_map/ppermute | solution.py:92
  79.7 5.8 %collective-permute-start.2 = (bf16[2,2,2048]{2,1,0:T(2,128)(2,1)S(1)}, bf16[2,2,2048]{2,1,0:T(2,128)(2,1)S(1)}, u32[]{:S(2)}, u32[]{:S(2)}) collective-permute-start(bf16[2,2,2048]{2,1,0:T(2,128)(2,1)S(1)} %collective-permute-done.1), channel_id=1, source_target_pairs={{0,4},{4,8},{8,12},{12,0},{1,5},{5,9},{9,13},{13,1},{2,6},{6,10},{... | collective-permute-start | bytes 49160 | tf_op jit(solution)/shard_map/ppermute | solution.py:92
Sparse Core Ops, SparseCore 0:
  16.4 37.3 all-reduce.8
  90.1 30.7 all-reduce.6
